TPU v7x, 32 devices: a whole 2x2x4 slice. The times are simulated.
32 devices in a mesh: gx: 4 (over x, core), gy: 4 (over z), gz: 2 (over y).
Axes of the slice: x: 2, y: 2, z: 4, core: 2. Of those that a mesh axis runs over, the one named last changes fastest.
Arguments:
- outcomes: bfloat16 [24576, 2048], P(('gx', 'gy', 'gz')), may hold values from -6 to 6
- sketch: bfloat16 [24576, 128], P(('gx', 'gy', 'gz')), may hold values from -6 to 6
Outputs:
- left_basis: float32 [24576, 128], P(('gx', 'gy', 'gz'))
- factor: float32 [128, 128], replicated
All inputs are finite; a program needn't handle non-finite values.
Results may differ from a plain program's by a relative error of at most 0.005.
Values may be sent and summed in bfloat16 or wider, within the bound.
A program may use at most 64 MiB of HBM per device.

v0:
```python
import math
import jax
import jax.numpy as jnp
from jax import lax
from jax.sharding import PartitionSpec as P

POWER = 2


def per_device(outcomes, sketch):
    device_count = lax.axis_size(("gx", "gy", "gz"))
    rows_here = outcomes.shape[0]
    day_count = outcomes.shape[1]
    unit_count = rows_here * device_count
    current = sketch
    left_basis = None
    lower_tri = None
    for power_step in range(POWER):
        partial_sum = lax.dot_general(
            outcomes, current, (((0,), (0,)), ((), ())), preferred_element_type=jnp.float32
        )
        summed = lax.psum(partial_sum, ("gx", "gy", "gz"))
        day_weights = (summed / math.sqrt(unit_count)).astype(jnp.bfloat16)
        projected = jnp.dot(outcomes, day_weights, preferred_element_type=jnp.float32)
        projected = projected / math.sqrt(day_count)
        gram_local = jnp.dot(projected.T, projected, precision=lax.Precision.HIGHEST) / unit_count
        gram = lax.psum(gram_local, ("gx", "gy", "gz"))
        lower_tri = jnp.linalg.cholesky(gram)
        left_basis = lax.linalg.triangular_solve(
            lower_tri, projected, left_side=False, lower=True, transpose_a=True
        )
        current = left_basis.astype(jnp.bfloat16)
    return (left_basis, lower_tri.T)


def solution(mesh):
    return jax.shard_map(
        per_device,
        mesh=mesh,
        in_specs=(P(("gx", "gy", "gz"), None), P(("gx", "gy", "gz"), None)),
        out_specs=(P(("gx", "gy", "gz"), None), P()),
        check_vma=False,
    )
```

profile of v0, /device:TPU:1, one launch (start us, length us, event | category | flops | bytes accessed | tf_op | source)
XLA Modules:
  0.0 607.3 jit_solution(11905937048318065328)
XLA Ops:
  7.2 0.0 copy-start
  7.2 0.0 all-reduce.5.cloned.1.call-start
  7.2 1.8 copy-done
  9.1 3.0 fusion.16
  12.0 0.0 all-reduce.5.cloned.1.call-update
  12.1 0.0 all-reduce.7.cloned.1.call-start
  12.1 133.1 %all-reduce.5.cloned.1.call-done = f32[2048,128]{1,0:T(8,128)} async-done(((f32[2048,128]{1,0:T(8,128)}), f32[2048,128]{1,0:T(8,128)}) %all-reduce.5.cloned.1.call-update) | async-done | bytes 1048592 | tf_op jit(solution)/shard_map/psum | solution.py:22
  145.2 2.4 convolution_multiply_fusion.1
  147.6 1.1 convolution_multiply_fusion.3
  148.7 0.0 all-reduce.7.cloned.1.call-update
  148.7 0.0 all-reduce.9.cloned.1.call-start
  148.8 123.7 %all-reduce.7.cloned.1.call-done = f32[128,128]{0,1:T(8,128)} async-done(((f32[128,128]{0,1:T(8,128)}), f32[128,128]{0,1:T(8,128)}) %all-reduce.7.cloned.1.call-update) | async-done | bytes 65552 | tf_op jit(solution)/shard_map/psum | solution.py:27
  272.5 1.6 copy.5
  274.0 1.5 fusion.9
  275.5 13.2 %cholesky.44 = f32[128,128]{1,0:T(8,128)} custom-call(f32[128,128]{1,0:T(8,128)} %fusion.9), custom_call_target="Cholesky" | custom-call | tf_op jit(solution)/shard_map/jit(cholesky)/cholesky | solution.py:28
  288.7 0.9 fusion.12
  289.6 0.6 compare_reduce_fusion.1
  290.2 2.1 fusion.5
  292.4 11.3 %custom-call.6 = f32[1,128,128]{1,2,0:T(8,128)} custom-call(f32[1,128,128]{2,1,0:T(8,128)} %fusion.5), custom_call_target="InvertDiagBlocksLowerTriangular" | custom-call | tf_op jit(solution)/shard_map/triangular_solve/custom-call.0 | solution.py:29
  303.6 1.3 fusion
  305.0 2.4 convolution_bitcast_fusion
  307.4 0.0 all-reduce.9.cloned.1.call-update
  307.4 0.2 all-reduce.11.cloned.1.call-start
  307.6 129.2 %all-reduce.9.cloned.1.call-done = f32[2048,128]{1,0:T(8,128)} async-done(((f32[2048,128]{1,0:T(8,128)}), f32[2048,128]{1,0:T(8,128)}) %all-reduce.9.cloned.1.call-update) | async-done | bytes 1048592 | tf_op jit(solution)/shard_map/psum | solution.py:22
  436.8 2.4 convolution_multiply_fusion
  439.2 1.1 convolution_multiply_fusion.2
  440.3 0.0 all-reduce.11.cloned.1.call-update
  440.4 123.6 %all-reduce.11.cloned.1.call-done = f32[128,128]{0,1:T(8,128)} async-done(((f32[128,128]{0,1:T(8,128)}), f32[128,128]{0,1:T(8,128)}) %all-reduce.11.cloned.1.call-update) | async-done | bytes 65552 | tf_op jit(solution)/shard_map/psum | solution.py:27
  564.0 1.6 copy.7
  565.5 1.5 fusion.7
  567.0 13.2 %cholesky.55 = f32[128,128]{1,0:T(8,128)} custom-call(f32[128,128]{1,0:T(8,128)} %fusion.7), custom_call_target="Cholesky" | custom-call | tf_op jit(solution)/shard_map/jit(cholesky)/cholesky | solution.py:28
  580.2 0.9 select_reduce_fusion
  581.1 0.6 compare_reduce_fusion
  581.7 2.1 fusion.13
  583.9 1.6 copy.9
  585.4 11.3 %custom-call.7 = f32[1,128,128]{1,2,0:T(8,128)} custom-call(f32[1,128,128]{2,1,0:T(8,128)} %get-tuple-element.7), custom_call_target="InvertDiagBlocksLowerTriangular" | custom-call | tf_op jit(solution)/shard_map/triangular_solve/custom-call.0 | solution.py:29
  596.7 2.1 convolution_bitcast_fusion.1
  598.8 1.9 copy.8
Async XLA Ops:
  7.2 1.9 copy-start
  7.2 138.0 %all-reduce.5.cloned.1.call-start = ((), (), s32[]{:S(2)}) async-start(), calls=%async_computation | async-start | bytes 2097152 | tf_op jit(solution)/shard_map/psum | solution.py:22
  12.1 260.4 %all-reduce.7.cloned.1.call-start = ((), (), s32[]{:S(2)}) async-start(), calls=%async_computation.1 | async-start | bytes 131072 | tf_op jit(solution)/shard_map/psum | solution.py:27
  148.7 288.1 %all-reduce.9.cloned.1.call-start = ((), (), s32[]{:S(2)}) async-start(), calls=%async_computation.2 | async-start | bytes 2097152 | tf_op jit(solution)/shard_map/psum | solution.py:22
  307.4 256.6 %all-reduce.11.cloned.1.call-start = ((), (), s32[]{:S(2)}) async-start(), calls=%async_computation.3 | async-start | bytes 131072 | tf_op jit(solution)/shard_map/psum | solution.py:27
Sparse Core Ops, SparseCore 0:
  13.2 131.9 all-reduce.4
  151.3 121.1 all-reduce.6
  307.5 129.2 all-reduce.8
  442.8 121.1 all-reduce.10
where the time goes:
time: 608 us; the launch traced here: 607 us
  waiting for transfers between devices  510 us (84%)
  other arithmetic  59.2 us (10%)
  matrix products  15.8 us (3%)
  between operations  13.8 us (2%)
  local copies, waits for them, and re-layouts  8.45 us (1%)
    psum x2, waiting for transfers between devices, per_device(): summed = lax.psum(partial_sum, ('gx', 'gy', 'gz'))  262 us
    psum x2, waiting for transfers between devices, per_device(): gram = lax.psum(gram_local, ('gx', 'gy', 'gz'))  247 us
    another operation x6, other arithmetic, per_device(): lower_tri = jnp.linalg.cholesky(gram)  29.4 us
    another operation x3, other arithmetic, per_device(): lax.linalg.triangular_solve(lower_tri, projected, left_side=False, lower=...  24.7 us
  transfers between devices with their start and end apart: 4, of which 4 were waited for; matrix products, arithmetic and copies ran while one was open for 0% of the time, Pallas kernels for 0%

commit v1 on v0

--- a/solution.py
+++ b/solution.py
@@ -24,7 +24,7 @@
         projected = jnp.dot(outcomes, day_weights, preferred_element_type=jnp.float32)
         projected = projected / math.sqrt(day_count)
         gram_local = jnp.dot(projected.T, projected, precision=lax.Precision.HIGHEST) / unit_count
-        gram = lax.psum(gram_local, ("gx", "gy", "gz"))
+        gram = jnp.sum(lax.all_gather(gram_local, ("gx", "gy", "gz")), axis=0)
         lower_tri = jnp.linalg.cholesky(gram)
         left_basis = lax.linalg.triangular_solve(
             lower_tri, projected, left_side=False, lower=True, transpose_a=True

time: 608 us -> 478 us (0.79)
  waiting for transfers between devices: 510 us -> 375 us
    psum x2 -> x0, waiting for transfers between devices: 247 us -> none  [per_device(): gram = lax.psum(gram_local, ('gx', 'gy', 'gz'))]
    all_gather x0 -> x2, waiting for transfers between devices: none -> 113 us  [per_device(): gram = jnp.sum(lax.all_gather(gram_local, ('gx', 'gy', 'gz')), axis=0)]
where the time goes in v1:
time: 478 us; the launch traced here: 477 us
  waiting for transfers between devices  375 us (78%)
  other arithmetic  63.9 us (13%)
  matrix products  15.8 us (3%)
  between operations  13.8 us (3%)
  local copies, waits for them, and re-layouts  8.45 us (2%)
    psum x2, waiting for transfers between devices, per_device(): summed = lax.psum(partial_sum, ('gx', 'gy', 'gz'))  261 us
    all_gather x2, waiting for transfers between devices, per_device(): gram = jnp.sum(lax.all_gather(gram_local, ('gx', 'gy', 'gz')), axis=0)  113 us
    another operation x6, other arithmetic, per_device(): lower_tri = jnp.linalg.cholesky(gram)  29.4 us
    another operation x3, other arithmetic, per_device(): lax.linalg.triangular_solve(lower_tri, projected, left_side=False, lower=...  24.7 us
  transfers between devices with their start and end apart: 4, of which 4 were waited for; matrix products, arithmetic and copies ran while one was open for 0% of the time, Pallas kernels for 0%

profile of v1, /device:TPU:1, one launch (start us, length us, event | category | flops | bytes accessed | tf_op | source)
XLA Modules:
  0.0 477.1 jit_solution(18086389481217033530)
XLA Ops:
  7.2 0.0 copy-start
  7.2 0.0 all-reduce.3.cloned.1.call-start
  7.2 1.8 copy-done
  9.1 3.0 fusion.16
  12.0 0.0 all-reduce.3.cloned.1.call-update
  12.1 0.0 all-gather.5.cloned.1.call-start
  12.1 133.1 %all-reduce.3.cloned.1.call-done = f32[2048,128]{1,0:T(8,128)} async-done(((f32[2048,128]{1,0:T(8,128)}), f32[2048,128]{1,0:T(8,128)}) %all-reduce.3.cloned.1.call-update) | async-done | bytes 1048592 | tf_op jit(solution)/shard_map/psum | solution.py:22
  145.2 2.4 convolution_multiply_fusion.1
  147.6 1.1 convolution_multiply_fusion.3
  148.7 0.0 all-gather.5.cloned.1.call-update
  148.7 0.0 all-reduce.5.cloned.1.call-start
  148.8 56.7 %all-gather.5.cloned.1.call-done = f32[4096,128]{1,0:T(8,128)} async-done(((f32[128,128]{1,0:T(8,128)}), f32[4096,128]{1,0:T(8,128)}) %all-gather.5.cloned.1.call-update) | async-done | bytes 2097168 | tf_op jit(solution)/shard_map/all_gather | solution.py:27
  205.4 2.3 reduce_sum.18
  207.8 1.6 copy.8
  209.3 1.5 fusion.9
  210.8 13.2 %cholesky.44 = f32[128,128]{1,0:T(8,128)} custom-call(f32[128,128]{1,0:T(8,128)} %fusion.9), custom_call_target="Cholesky" | custom-call | tf_op jit(solution)/shard_map/jit(cholesky)/cholesky | solution.py:28
  224.0 0.9 fusion.12
  224.9 0.6 compare_reduce_fusion.1
  225.5 2.1 fusion.5
  227.7 11.3 %custom-call.6 = f32[1,128,128]{1,2,0:T(8,128)} custom-call(f32[1,128,128]{2,1,0:T(8,128)} %fusion.5), custom_call_target="InvertDiagBlocksLowerTriangular" | custom-call | tf_op jit(solution)/shard_map/triangular_solve/custom-call.0 | solution.py:29
  238.9 1.4 fusion
  240.3 2.4 convolution_bitcast_fusion
  242.7 0.0 all-reduce.5.cloned.1.call-update
  242.7 0.2 all-gather.7.cloned.1.call-start
  242.9 128.3 %all-reduce.5.cloned.1.call-done = f32[2048,128]{1,0:T(8,128)} async-done(((f32[2048,128]{1,0:T(8,128)}), f32[2048,128]{1,0:T(8,128)}) %all-reduce.5.cloned.1.call-update) | async-done | bytes 1048592 | tf_op jit(solution)/shard_map/psum | solution.py:22
  371.2 2.4 convolution_multiply_fusion
  373.6 1.1 convolution_multiply_fusion.2
  374.7 0.0 all-gather.7.cloned.1.call-update
  374.8 56.7 %all-gather.7.cloned.1.call-done = f32[4096,128]{1,0:T(8,128)} async-done(((f32[128,128]{1,0:T(8,128)}), f32[4096,128]{1,0:T(8,128)}) %all-gather.7.cloned.1.call-update) | async-done | bytes 2097168 | tf_op jit(solution)/shard_map/all_gather | solution.py:27
  431.5 2.3 reduce_sum.19
  433.8 1.6 copy.9
  435.4 1.5 fusion.7
  436.9 13.2 %cholesky.55 = f32[128,128]{1,0:T(8,128)} custom-call(f32[128,128]{1,0:T(8,128)} %fusion.7), custom_call_target="Cholesky" | custom-call | tf_op jit(solution)/shard_map/jit(cholesky)/cholesky | solution.py:28
  450.1 0.9 select_reduce_fusion
  450.9 0.6 compare_reduce_fusion
  451.6 2.1 fusion.13
  453.7 1.6 copy.11
  455.3 11.3 %custom-call.7 = f32[1,128,128]{1,2,0:T(8,128)} custom-call(f32[1,128,128]{2,1,0:T(8,128)} %get-tuple-element.9), custom_call_target="InvertDiagBlocksLowerTriangular" | custom-call | tf_op jit(solution)/shard_map/triangular_solve/custom-call.0 | solution.py:29
  466.6 2.1 convolution_bitcast_fusion.1
  468.7 1.9 copy.10
Async XLA Ops:
  7.2 1.9 copy-start
  7.2 138.0 %all-reduce.3.cloned.1.call-start = ((), (), s32[]{:S(2)}) async-start(), calls=%async_computation | async-start | bytes 2097152 | tf_op jit(solution)/shard_map/psum | solution.py:22
  12.1 193.4 %all-gather.5.cloned.1.call-start = ((), (), s32[]{:S(2)}) async-start(), calls=%async_computation.2 | async-start | bytes 2162688 | tf_op jit(solution)/shard_map/all_gather | solution.py:27
  148.7 222.5 %all-reduce.5.cloned.1.call-start = ((), (), s32[]{:S(2)}) async-start(), calls=%async_computation.1 | async-start | bytes 2097152 | tf_op jit(solution)/shard_map/psum | solution.py:22
  242.7 188.8 %all-gather.7.cloned.1.call-start = ((), (), s32[]{:S(2)}) async-start(), calls=%async_computation.3 | async-start | bytes 2162688 | tf_op jit(solution)/shard_map/all_gather | solution.py:27
Sparse Core Ops, SparseCore 0:
  13.2 131.9 all-reduce.2
  148.8 56.5 all-gather.4
  242.8 128.3 all-reduce.4
  374.9 56.5 all-gather.6

commit v2 on v0

--- a/solution.py
+++ b/solution.py
@@ -24,7 +24,7 @@
         projected = jnp.dot(outcomes, day_weights, preferred_element_type=jnp.float32)
         projected = projected / math.sqrt(day_count)
         gram_local = jnp.dot(projected.T, projected, precision=lax.Precision.HIGHEST) / unit_count
-        gram = lax.psum(gram_local, ("gx", "gy", "gz"))
+        gram = lax.psum(lax.psum(gram_local, ("gy", "gz")), "gx")
         lower_tri = jnp.linalg.cholesky(gram)
         left_basis = lax.linalg.triangular_solve(
             lower_tri, projected, left_side=False, lower=True, transpose_a=True

time: 608 us -> 569 us (0.936)
  waiting for transfers between devices: 510 us -> 468 us
    psum x2 -> x4, waiting for transfers between devices: 247 us -> 203 us  [per_device(): gram = lax.psum(lax.psum(gram_local, ('gy', 'gz')), 'gx')]
  transfers between devices with their start and end apart: 4 -> 6, of which waited for: 4 -> 6; matrix products, arithmetic and copies ran while one was open for 0% -> 0% of each run, Pallas kernels for 0% -> 0%
where the time goes in v2:
time: 569 us; the launch traced here: 566 us
  waiting for transfers between devices  468 us (82%)
  other arithmetic  59.2 us (10%)
  matrix products  15.8 us (3%)
  between operations  14.1 us (2%)
  local copies, waits for them, and re-layouts  8.45 us (1%)
    psum x2, waiting for transfers between devices, per_device(): summed = lax.psum(partial_sum, ('gx', 'gy', 'gz'))  264 us
    psum x4, waiting for transfers between devices, per_device(): gram = lax.psum(lax.psum(gram_local, ('gy', 'gz')), 'gx')  203 us
    another operation x6, other arithmetic, per_device(): lower_tri = jnp.linalg.cholesky(gram)  29.4 us
    another operation x3, other arithmetic, per_device(): lax.linalg.triangular_solve(lower_tri, projected, left_side=False, lower=...  24.7 us
  transfers between devices with their start and end apart: 6, of which 6 were waited for; matrix products, arithmetic and copies ran while one was open for 0% of the time, Pallas kernels for 0%

profile of v2, /device:TPU:1, one launch (start us, length us, event | category | flops | bytes accessed | tf_op | source)
XLA Modules:
  0.0 565.8 jit_solution(15883863701231694764)
XLA Ops:
  7.2 0.0 copy-start
  7.2 0.0 all-reduce.7.cloned.1.call-start
  7.2 1.8 copy-done
  9.1 3.0 fusion.16
  12.0 0.0 all-reduce.7.cloned.1.call-update
  12.1 0.0 all-reduce.9.cloned.1.call-start
  12.1 133.1 %all-reduce.7.cloned.1.call-done = f32[2048,128]{1,0:T(8,128)} async-done(((f32[2048,128]{1,0:T(8,128)}), f32[2048,128]{1,0:T(8,128)}) %all-reduce.7.cloned.1.call-update) | async-done | bytes 1048592 | tf_op jit(solution)/shard_map/psum | solution.py:22
  145.2 2.4 convolution_multiply_fusion.1
  147.6 1.1 convolution_multiply_fusion.3
  148.7 0.0 all-reduce.9.cloned.1.call-update
  148.7 0.0 all-reduce.11.cloned.1.call-start
  148.8 67.6 %all-reduce.9.cloned.1.call-done = f32[128,128]{0,1:T(8,128)} async-done(((f32[128,128]{0,1:T(8,128)}), f32[128,128]{0,1:T(8,128)}) %all-reduce.9.cloned.1.call-update) | async-done | bytes 65552 | tf_op jit(solution)/shard_map/psum | solution.py:27
  216.4 0.0 all-reduce.11.cloned.1.call-update
  216.4 0.0 all-reduce.13.cloned.1.call-start
  216.5 34.1 %all-reduce.11.cloned.1.call-done = f32[128,128]{0,1:T(8,128)} async-done(((f32[128,128]{0,1:T(8,128)}), f32[128,128]{0,1:T(8,128)}) %all-reduce.11.cloned.1.call-update) | async-done | bytes 65552 | tf_op jit(solution)/shard_map/psum | solution.py:27
  250.6 1.6 copy.5
  252.2 1.5 fusion.9
  253.7 13.2 %cholesky.44 = f32[128,128]{1,0:T(8,128)} custom-call(f32[128,128]{1,0:T(8,128)} %fusion.9), custom_call_target="Cholesky" | custom-call | tf_op jit(solution)/shard_map/jit(cholesky)/cholesky | solution.py:28
  266.9 0.9 fusion.12
  267.7 0.6 compare_reduce_fusion.1
  268.4 2.1 fusion.5
  270.5 11.3 %custom-call.6 = f32[1,128,128]{1,2,0:T(8,128)} custom-call(f32[1,128,128]{2,1,0:T(8,128)} %fusion.5), custom_call_target="InvertDiagBlocksLowerTriangular" | custom-call | tf_op jit(solution)/shard_map/triangular_solve/custom-call.0 | solution.py:29
  281.8 1.3 fusion
  283.1 2.4 convolution_bitcast_fusion
  285.5 0.0 all-reduce.13.cloned.1.call-update
  285.5 0.0 all-reduce.15.cloned.1.call-start
  285.6 131.4 %all-reduce.13.cloned.1.call-done = f32[2048,128]{1,0:T(8,128)} async-done(((f32[2048,128]{1,0:T(8,128)}), f32[2048,128]{1,0:T(8,128)}) %all-reduce.13.cloned.1.call-update) | async-done | bytes 1048592 | tf_op jit(solution)/shard_map/psum | solution.py:22
  417.0 2.4 convolution_multiply_fusion
  419.4 1.1 convolution_multiply_fusion.2
  420.6 0.0 all-reduce.15.cloned.1.call-update
  420.6 0.2 all-reduce.17.cloned.1.call-start
  420.8 67.3 %all-reduce.15.cloned.1.call-done = f32[128,128]{0,1:T(8,128)} async-done(((f32[128,128]{0,1:T(8,128)}), f32[128,128]{0,1:T(8,128)}) %all-reduce.15.cloned.1.call-update) | async-done | bytes 65552 | tf_op jit(solution)/shard_map/psum | solution.py:27
  488.1 0.0 all-reduce.17.cloned.1.call-update
  488.1 34.0 %all-reduce.17.cloned.1.call-done = f32[128,128]{0,1:T(8,128)} async-done(((f32[128,128]{0,1:T(8,128)}), f32[128,128]{0,1:T(8,128)}) %all-reduce.17.cloned.1.call-update) | async-done | bytes 65552 | tf_op jit(solution)/shard_map/psum | solution.py:27
  522.2 1.6 copy.7
  523.7 1.5 fusion.7
  525.2 13.2 %cholesky.55 = f32[128,128]{1,0:T(8,128)} custom-call(f32[128,128]{1,0:T(8,128)} %fusion.7), custom_call_target="Cholesky" | custom-call | tf_op jit(solution)/shard_map/jit(cholesky)/cholesky | solution.py:28
  538.4 0.9 select_reduce_fusion
  539.3 0.6 compare_reduce_fusion
  539.9 2.1 fusion.13
  542.1 1.6 copy.9
  543.6 11.3 %custom-call.7 = f32[1,128,128]{1,2,0:T(8,128)} custom-call(f32[1,128,128]{2,1,0:T(8,128)} %get-tuple-element.7), custom_call_target="InvertDiagBlocksLowerTriangular" | custom-call | tf_op jit(solution)/shard_map/triangular_solve/custom-call.0 | solution.py:29
  554.9 2.1 convolution_bitcast_fusion.1
  557.0 1.9 copy.8
Async XLA Ops:
  7.2 1.9 copy-start
  7.2 138.0 %all-reduce.7.cloned.1.call-start = ((), (), s32[]{:S(2)}) async-start(), calls=%async_computation | async-start | bytes 2097152 | tf_op jit(solution)/shard_map/psum | solution.py:22
  12.1 204.3 %all-reduce.9.cloned.1.call-start = ((), (), s32[]{:S(2)}) async-start(), calls=%async_computation.1 | async-start | bytes 131072 | tf_op jit(solution)/shard_map/psum | solution.py:27
  148.7 101.9 %all-reduce.11.cloned.1.call-start = ((), (), s32[]{:S(2)}) async-start(), calls=%async_computation.2 | async-start | bytes 131072 | tf_op jit(solution)/shard_map/psum | solution.py:27
  216.4 200.6 %all-reduce.13.cloned.1.call-start = ((), (), s32[]{:S(2)}) async-start(), calls=%async_computation.3 | async-start | bytes 2097152 | tf_op jit(solution)/shard_map/psum | solution.py:22
  285.5 202.6 %all-reduce.15.cloned.1.call-start = ((), (), s32[]{:S(2)}) async-start(), calls=%async_computation.4 | async-start | bytes 131072 | tf_op jit(solution)/shard_map/psum | solution.py:27
  420.6 101.6 %all-reduce.17.cloned.1.call-start = ((), (), s32[]{:S(2)}) async-start(), calls=%async_computation.5 | async-start | bytes 131072 | tf_op jit(solution)/shard_map/psum | solution.py:27
Sparse Core Ops, SparseCore 0:
  13.2 131.9 all-reduce.6
  149.1 67.1 all-reduce.8
  218.7 31.8 all-reduce.10
  285.7 131.3 all-reduce.12
  420.9 67.1 all-reduce.14
  490.3 31.8 all-reduce.16
